TPU v7x, 32 devices: a whole 2x2x4 slice. The times are simulated.
32 devices in a mesh: row: 4 (over x, core), col: 8 (over z, y).
Axes of the slice: x: 2, y: 2, z: 4, core: 2. Of those that a mesh axis runs over, the one named last changes fastest.
Arguments:
- rows: bfloat16 [1024, 4096], P(('row', 'col')), may hold values from -6 to 6
- task_ids: int32 [1024], P(('row', 'col')), may hold values from 0 to 8, as said below
- task_embed: bfloat16 [8, 4096], replicated, may hold values from -6 to 6
- norm_gain: float32 [4, 4096], replicated, may hold values from 0.1 to 1.9
- layer_weight: bfloat16 [4, 4096, 4096], P(None, None, 'col'), may hold values from -0.09375 to 0.09375
Outputs:
- packed_out: bfloat16 [1024, 4096], P('row', 'col')
Inputs may be any that keep to these rules, and one draw needn't show every extreme that they name: `task_ids`: 8 marks an empty row, smaller values name a task.
All inputs are finite; a program needn't handle non-finite values.
Results may differ from a plain program's by a relative error of at most 0.008.
Values may be sent and summed in bfloat16 or wider, within the bound.
A program may use at most 128 MiB of HBM per device.

v0:
```python
import jax
import jax.numpy as jnp
from jax import lax
from jax.sharding import PartitionSpec as P

epsilon = 1e-06


def entering(part, axis, combine, identity):
    place = lax.axis_index(axis)
    gathered = lax.all_gather(part, axis)
    state = jnp.zeros_like(part) + jnp.asarray(identity, part.dtype)

    def one(hop, state):
        return combine(state, lax.dynamic_index_in_dim(gathered, hop, 0, False))

    return lax.fori_loop(0, place, one, state)


def add_counts(earlier, later):
    return earlier + later


def activate_rows(hidden, gain):
    total_rows = hidden.shape[0]
    width = hidden.shape[1]
    block_rows = min(512, total_rows)

    def one_block(block):
        values = block.astype(jnp.float32)
        inverse_rms = lax.rsqrt(jnp.mean(values * values, axis=1, keepdims=True) + epsilon)
        return jax.nn.silu(values * inverse_rms * gain[None, :]).astype(jnp.bfloat16)

    blocks = hidden.reshape(total_rows // block_rows, block_rows, width)
    return lax.map(one_block, blocks).reshape(total_rows, width)


def shards(rows, task_ids, task_embed, norm_gain, layer_weight):
    row_count = rows.shape[0]
    width = rows.shape[1]
    task_count = task_embed.shape[0]
    row_devices = lax.axis_size("row")
    col_devices = lax.axis_size("col")
    capacity = row_count // row_devices + task_count
    slots_group = row_count * col_devices
    task_range = jnp.arange(task_count, dtype=jnp.int32)
    member = (task_ids[:, None] == task_range[None, :]).astype(jnp.int32)
    counts = jnp.sum(member, axis=0)
    zero_counts = jnp.zeros_like(counts)
    before_col = entering(counts, "col", add_counts, zero_counts)
    row_total = lax.psum(counts, "col")
    before_row = entering(row_total, "row", add_counts, zero_counts)
    totals = lax.psum(row_total, "row")
    before = before_row + before_col
    task_base = jnp.cumsum(totals) - totals
    positions = jnp.arange(row_count, dtype=jnp.int32)
    earlier_mask = positions[None, :] < positions[:, None]
    same_task = task_ids[:, None] == task_ids[None, :]
    task_rank = jnp.sum((same_task & earlier_mask).astype(jnp.int32), axis=1)
    row_live = task_ids < task_count
    packed_pos = (
        jnp.sum(member * (task_base + before)[None, :], axis=1).astype(jnp.int32) + task_rank
    )
    target_row = packed_pos % row_devices
    slot_index = packed_pos // row_devices
    before_pos = packed_pos[None, :] < packed_pos[:, None]
    same_target = (target_row[:, None] == target_row[None, :]) & row_live[None, :]
    within = jnp.sum((same_target & before_pos).astype(jnp.int32), axis=1)
    send_at = jnp.where(row_live, target_row * capacity + within, -1)
    buffer_range = jnp.arange(row_devices * capacity, dtype=jnp.int32)
    select = buffer_range[:, None] == send_at[None, :]
    send_rows = jnp.dot(
        select.astype(jnp.bfloat16), rows, preferred_element_type=jnp.float32
    ).astype(jnp.bfloat16)
    send_rows = send_rows.reshape(row_devices, capacity, width)
    send_slots = jnp.sum(jnp.where(select, slot_index[None, :] + 1, 0), axis=1) - 1
    send_slots = send_slots.reshape(row_devices, capacity)
    got_rows, got_slots = (
        lax.all_to_all(send_rows, "row", split_axis=0, concat_axis=0, tiled=True),
        lax.all_to_all(send_slots, "row", split_axis=0, concat_axis=0, tiled=True),
    )
    got_rows = got_rows.reshape(row_devices * capacity, width)
    got_slots = got_slots.reshape(row_devices * capacity)
    slot_range = jnp.arange(slots_group, dtype=jnp.int32)
    piece_rows = lax.all_gather(got_rows, "col", axis=0, tiled=True)
    piece_slots = lax.all_gather(got_slots, "col", axis=0, tiled=True)
    safe_slots = jnp.where(piece_slots >= 0, piece_slots, slots_group).astype(jnp.int32)
    placed = (
        jnp.zeros((slots_group, width), jnp.bfloat16).at[safe_slots].set(piece_rows, mode="drop")
    )
    group_index = lax.axis_index("row")
    slot_pos = slot_range * row_devices + group_index
    in_task = (slot_pos[:, None] >= task_base[None, :]) & (
        slot_pos[:, None] < (task_base + totals)[None, :]
    )
    task_term = jnp.dot(
        in_task.astype(jnp.bfloat16), task_embed, preferred_element_type=jnp.float32
    )
    hidden = (placed.astype(jnp.float32) + task_term).astype(jnp.bfloat16)
    part_width = width // col_devices
    column = lax.axis_index("col") * part_width
    layers = layer_weight.shape[0]
    result = hidden
    for layer_index in range(layers):
        active = activate_rows(hidden, norm_gain[layer_index])
        update = jnp.dot(active, layer_weight[layer_index], preferred_element_type=jnp.float32)
        own_cols = lax.dynamic_slice_in_dim(hidden, column, part_width, 1).astype(jnp.float32)
        result = (own_cols + update).astype(jnp.bfloat16)
        if layer_index + 1 < layers:
            hidden = lax.all_gather(result, "col", axis=1, tiled=True)
    return result


def solution(mesh):
    return jax.shard_map(
        shards,
        mesh=mesh,
        in_specs=(P(("row", "col"), None), P(("row", "col")), P(), P(), P(None, None, "col")),
        out_specs=P("row", "col"),
        check_vma=False,
    )
```

profile of v0, /device:TPU:0, one launch (start us, length us, event | category | flops | bytes accessed | tf_op | source)
XLA Modules:
  0.0 303.9 jit_solution(6992512767991493794)
XLA Ops:
  6.5 0.8 convert_reduce_fusion.2
  7.4 0.9 convert_reduce_fusion.1
  8.3 0.7 broadcast_compare_fusion
  8.9 1.3 dynamic-slice.5
  10.9 0.2 dynamic-update-slice.1
  11.1 13.1 %all-reduce.3 = (s32[8]{0:T(128)S(1)}, s32[64]{0:T(128)S(1)}) all-reduce(s32[8]{0:T(128)S(1)} %convert_reduce_fusion.2, s32[64]{0:T(128)S(1)} %dynamic-update-slice.1), channel_id=1, replica_groups=mesh['row'=4,'col'=8] {'col'}, use_global_device_ids=true, to_apply=%region_1.2 | all-reduce | flops 72 | bytes 576 | tf_op jit(solution)/shard_map/psum | solution.py:51
  24.2 1.2 dynamic-slice.4
  26.4 4.9 %all-reduce.4 = (s32[8]{0:T(128)S(1)}, s32[32]{0:T(128)S(1)}) all-reduce(s32[8]{0:T(128)S(1)} %get-tuple-element.117, s32[32]{0:T(128)S(1)} %dynamic-update-slice), channel_id=1, replica_groups=mesh['row'=4,'col'=8] {'row'}, use_global_device_ids=true, to_apply=%region_2.3 | all-reduce | flops 40 | bytes 320 | tf_op jit(solution)/shard_map/psum | solution.py:53
  31.6 0.7 select_reduce_fusion.1
  32.6 0.7 add_select_fusion
  33.2 0.4 convolution_convert_fusion
  33.7 11.9 %all_to_all.11 = bf16[4,16,4096]{2,1,0:T(8,128)(2,1)} all-to-all(bf16[4,16,4096]{2,1,0:T(8,128)(2,1)S(1)} %bitcast.53), channel_id=1, replica_groups=mesh['row'=4,'col'=8] {'row'}, dimensions={0} | all-to-all | bytes 1048576 | tf_op jit(solution)/shard_map/all_to_all | solution.py:79
  45.7 0.7 sub.18
  46.3 3.2 %all-to-all-start = ((s32[4,1,16]{2,1,0:T(1,128)}), s32[4,1,16]{2,1,0:T(1,128)S(1)}, u32[]{:S(2)}, u32[]{:S(2)}) async-start(s32[4,1,16]{2,1,0:T(1,128)} %bitcast.6), calls=%async_computation | async-start | bytes 4096 | tf_op jit(solution)/shard_map/all_to_all | solution.py:80
  50.3 1.1 fusion.112
  51.3 1.9 all-to-all-done
  53.2 0.5 broadcast.253
  53.8 0.7 reduce.3
  54.7 9.3 %all-reduce.2 = s32[512]{0:T(512)S(1)} all-reduce(s32[512]{0:T(512)S(1)} %dynamic-update-slice.2), channel_id=1, replica_groups=mesh['row'=4,'col'=8] {'col'}, use_global_device_ids=true, to_apply=%add.2 | all-reduce | flops 512 | bytes 4096
  64.0 52.0 %all-gather.7.cloned.1.call-done = bf16[512,4096]{1,0:T(8,128)(2,1)} async-done(((bf16[64,4096]{1,0:T(8,128)(2,1)}), bf16[512,4096]{1,0:T(8,128)(2,1)}) %all-gather.7.cloned.1.call-update) | async-done | bytes 4194320 | tf_op jit(solution)/shard_map/all_gather | solution.py:85
  116.0 8.2 %scatter_custom_fusion = bf16[256,4096]{1,0:T(8,128)(2,1)S(1)} fusion(s32[512]{0:T(512)S(1)} %compare_select_fusion, bf16[512,4096]{1,0:T(8,128)(2,1)} %all-gather.7.cloned.1.call-done, bf16[]{:T(256)} %constant.131.clone.1), kind=kCustom, calls=%fused_computation.74 | custom fusion | bytes 2097664 | tf_op jit(solution)/shard_map/scatter | solution.py:89
  124.3 1.0 fusion.1
  125.3 4.4 %fusion.92 = bf16[256,512]{1,0:T(8,128)(2,1)} fusion(bf16[4,4096,512]{2,1,0:T(8,128)(2,1)} %param.13, bf16[256,4096]{1,0:T(8,128)(2,1)S(1)} %get-tuple-element.130, f32[4096]{0:T(1024)S(1)} %bitcast.57, f32[256]{0:T(256)S(1)} %add_rsqrt_fusion.3, s32[]{:T(128)S(6)} %select_n.59), kind=kOutput, calls=%fused_computation.73 | convolution fusion | flops 1082523648 | bytes 6833156 | tf_op jit(solution)/shard_map/dot_general | solution.py:106
  129.9 48.8 %all-gather.9.cloned.1.call-done = bf16[256,4096]{1,0:T(8,128)(2,1)} async-done(((bf16[256,512]{1,0:T(8,128)(2,1)}), bf16[256,4096]{1,0:T(8,128)(2,1)}) %all-gather.9.cloned.1.call-update) | async-done | bytes 2097168 | tf_op jit(solution)/shard_map/all_gather | solution.py:110
  178.7 2.1 fusion.9
  180.8 5.0 %fusion.87 = bf16[256,512]{1,0:T(8,128)(2,1)} fusion(bf16[4,4096,512]{2,1,0:T(8,128)(2,1)} %param.13, bf16[256,4096]{1,0:T(8,128)(2,1)} %all-gather.9.cloned.1.call-done, f32[4096]{0:T(1024)S(1)} %bitcast.56, f32[256]{0:T(256)S(1)} %add_rsqrt_fusion.2, s32[]{:T(128)S(6)} %select_n.59), kind=kOutput, calls=%fused_computation.72 | convolution fusion | flops 1082523648 | bytes 6833156 | tf_op jit(solution)/shard_map/dot_general | solution.py:106
  185.8 48.6 %all-gather.11.cloned.1.call-done = bf16[256,4096]{1,0:T(8,128)(2,1)} async-done(((bf16[256,512]{1,0:T(8,128)(2,1)}), bf16[256,4096]{1,0:T(8,128)(2,1)}) %all-gather.11.cloned.1.call-update) | async-done | bytes 2097168 | tf_op jit(solution)/shard_map/all_gather | solution.py:110
  234.5 2.1 fusion.17
  236.6 5.0 %fusion.82 = bf16[256,512]{1,0:T(8,128)(2,1)} fusion(bf16[4,4096,512]{2,1,0:T(8,128)(2,1)} %param.13, bf16[256,4096]{1,0:T(8,128)(2,1)} %all-gather.11.cloned.1.call-done, f32[4096]{0:T(1024)S(1)} %bitcast.55, f32[256]{0:T(256)S(1)} %add_rsqrt_fusion.1, s32[]{:T(128)S(6)} %select_n.59), kind=kOutput, calls=%fused_computation.71 | convolution fusion | flops 1082523648 | bytes 6833156 | tf_op jit(solution)/shard_map/dot_general | solution.py:106
  241.6 48.8 %all-gather.13.cloned.1.call-done = bf16[256,4096]{1,0:T(8,128)(2,1)} async-done(((bf16[256,512]{1,0:T(8,128)(2,1)}), bf16[256,4096]{1,0:T(8,128)(2,1)}) %all-gather.13.cloned.1.call-update) | async-done | bytes 2097168 | tf_op jit(solution)/shard_map/all_gather | solution.py:110
  290.3 2.1 fusion.25
  292.4 5.0 %fusion.77 = bf16[256,512]{1,0:T(8,128)(2,1)} fusion(bf16[4,4096,512]{2,1,0:T(8,128)(2,1)} %param.13, bf16[256,4096]{1,0:T(8,128)(2,1)} %all-gather.13.cloned.1.call-done, f32[4096]{0:T(1024)S(1)} %bitcast.54, f32[256]{0:T(256)S(1)} %add_rsqrt_fusion, s32[]{:T(128)S(6)} %select_n.59), kind=kOutput, calls=%fused_computation.70 | convolution fusion | flops 1082523648 | bytes 6833156 | tf_op jit(solution)/shard_map/dot_general | solution.py:106
  (36 shorter events, 1.6 us)
Async XLA Ops:
  6.5 26.7 %copy-start = (bf16[32,4096]{1,0:T(8,128)(2,1)S(1)}, bf16[32,4096]{1,0:T(8,128)(2,1)}, u32[]{:S(2)}) copy-start(bf16[32,4096]{1,0:T(8,128)(2,1)} %param.9) | copy-start | bytes 786436
  6.5 117.7 %copy-start.1 = (bf16[8,4096]{1,0:T(8,128)(2,1)S(1)}, bf16[8,4096]{1,0:T(8,128)(2,1)}, u32[]{:S(2)}) copy-start(bf16[8,4096]{1,0:T(8,128)(2,1)} %param.11) | copy-start | bytes 196612
  6.5 109.5 %all-gather.7.cloned.1.call-start = ((), (), s32[]{:S(2)}) async-start(), calls=%async_computation.2 | async-start | bytes 4718592 | tf_op jit(solution)/shard_map/all_gather | solution.py:85
  46.3 6.9 %all-to-all-start = ((s32[4,1,16]{2,1,0:T(1,128)}), s32[4,1,16]{2,1,0:T(1,128)S(1)}, u32[]{:S(2)}, u32[]{:S(2)}) async-start(s32[4,1,16]{2,1,0:T(1,128)} %bitcast.6), calls=%async_computation | async-start | bytes 4096 | tf_op jit(solution)/shard_map/all_to_all | solution.py:80
  49.6 129.1 %all-gather.9.cloned.1.call-start = ((), (), s32[]{:S(2)}) async-start(), calls=%async_computation.3 | async-start | bytes 2359296 | tf_op jit(solution)/shard_map/all_gather | solution.py:110
  129.7 104.8 %all-gather.11.cloned.1.call-start = ((), (), s32[]{:S(2)}) async-start(), calls=%async_computation.4 | async-start | bytes 2359296 | tf_op jit(solution)/shard_map/all_gather | solution.py:110
  185.8 104.5 %all-gather.13.cloned.1.call-start = ((), (), s32[]{:S(2)}) async-start(), calls=%async_computation.5 | async-start | bytes 2359296 | tf_op jit(solution)/shard_map/all_gather | solution.py:110
Sparse Core Ops, SparseCore 0:
  45.7 70.2 all-gather.6
  129.8 48.8 all-gather.8
  185.9 48.5 all-gather.10
  241.7 48.5 all-gather.12
where the time goes:
time: 304 us
  waiting for transfers between devices  200 us (66%)
  blocking collectives  39.2 us (13%)
  matrix products  20.7 us (7%)
  between operations  15.1 us (5%)
  local copies, waits for them, and re-layouts  13.9 us (5%)
  other arithmetic  11.3 us (4%)
  starting transfers between devices  3.53 us (1%)
    all_gather x3, waiting for transfers between devices, shards(): hidden = lax.all_gather(result, 'col', axis=1, tiled=True)  146 us
    all_gather x1, waiting for transfers between devices, shards(): piece_rows = lax.all_gather(got_rows, 'col', axis=0, tiled=True)  52 us
    dot_general x4, matrix products, shards(): jnp.dot(active, layer_weight[layer_index], preferred_element_type=jnp.flo...  19.3 us
    psum x1, blocking collectives, shards(): row_total = lax.psum(counts, 'col')  13.1 us
    all_to_all x1, blocking collectives, shards(): lax.all_to_all(send_rows, 'row', split_axis=0, concat_axis=0, tiled=True)  11.9 us
    unnamed x1, blocking collectives  9.34 us
    scatter x1, local copies, waits for them, and re-layouts, shards(): jnp.zeros((slots_group, width), jnp.bfloat16).at[safe_slots]  8.22 us
    reduce_sum x3, other arithmetic, one_block(): jnp.mean(values * values, axis=1, keepdims=True) + epsilon  6.25 us
  transfers between devices with their start and end apart: 5, of which 5 were waited for; matrix products, arithmetic and copies ran while one was open for 1% of the time, Pallas kernels for 0%

commit v1 on v0

--- a/solution.py
+++ b/solution.py
@@ -4,6 +4,24 @@
 from jax.sharding import PartitionSpec as P
 
 epsilon = 1e-06
+
+
+def ring_gather(array, axis, dim):
+    ways, here, step = (lax.axis_size(axis), lax.axis_index(axis), array.shape[dim])
+    shape = [n * ways if d == dim else n for d, n in enumerate(array.shape)]
+    full = lax.dynamic_update_slice_in_dim(
+        jnp.zeros(shape, array.dtype), array, here * step, axis=dim
+    )
+    going_up = going_down = array
+    for far in range(1, ways // 2 + 1):
+        going_up = lax.ppermute(going_up, axis, [(d, (d + 1) % ways) for d in range(ways)])
+        full = lax.dynamic_update_slice_in_dim(full, going_up, (here - far) % ways * step, axis=dim)
+        if 2 * far < ways:
+            going_down = lax.ppermute(going_down, axis, [(d, (d - 1) % ways) for d in range(ways)])
+            full = lax.dynamic_update_slice_in_dim(
+                full, going_down, (here + far) % ways * step, axis=dim
+            )
+    return full
 
 
 def entering(part, axis, combine, identity):
@@ -82,7 +100,7 @@
     got_rows = got_rows.reshape(row_devices * capacity, width)
     got_slots = got_slots.reshape(row_devices * capacity)
     slot_range = jnp.arange(slots_group, dtype=jnp.int32)
-    piece_rows = lax.all_gather(got_rows, "col", axis=0, tiled=True)
+    piece_rows = ring_gather(got_rows, "col", 0)
     piece_slots = lax.all_gather(got_slots, "col", axis=0, tiled=True)
     safe_slots = jnp.where(piece_slots >= 0, piece_slots, slots_group).astype(jnp.int32)
     placed = (

time: 304 us -> 337 us (1.11)
  starting transfers between devices: 3.53 us -> 30.4 us
  blocking collectives: 39.2 us -> 26.4 us
  local copies, waits for them, and re-layouts: 13.9 us -> 23.2 us
  matrix products: 20.7 us -> 24.1 us
    ppermute x0 -> x7, waiting for transfers between devices: none -> 53.1 us  [the longest x3 39.1 us: ring_gather(): lax.ppermute(going_down, axis, [(d, (d - 1) % ways) for d in range(ways)])]
    all_gather x1 -> x0, waiting for transfers between devices: 52 us -> none  [shards(): piece_rows = lax.all_gather(got_rows, 'col', axis=0, tiled=True)]
    ppermute x0 -> x7, starting transfers between devices: none -> 23.6 us  [the longest x3 19.5 us: ring_gather(): lax.ppermute(going_down, axis, [(d, (d - 1) % ways) for d in range(ways)])]
    all_to_all x1 -> x0, blocking collectives: 11.9 us -> none  [shards(): lax.all_to_all(send_rows, 'row', split_axis=0, concat_axis=0, tiled=True)]
    dynamic_update_slice x0 -> x8, local copies, waits for them, and re-layouts: none -> 6.73 us  [the longest x4 3.37 us: ring_gather(): lax.dynamic_update_slice_in_dim(full, going_up, (here - far) % ways * ste...]
    all_to_all x0 -> x1, starting transfers between devices: none -> 3.47 us  [shards(): lax.all_to_all(send_rows, 'row', split_axis=0, concat_axis=0, tiled=True)]
    reduce_sum x3 -> x4, other arithmetic: 6.25 us -> 9.27 us  [one_block(): jnp.mean(values * values, axis=1, keepdims=True) + epsilon]
  transfers between devices with their start and end apart: 5 -> 12, of which waited for: 5 -> 7; matrix products, arithmetic and copies ran while one was open for 1% -> 5% of each run, Pallas kernels for 0% -> 0%
where the time goes in v1:
time: 337 us; the launch traced here: 336 us
  waiting for transfers between devices  203 us (60%)
  starting transfers between devices  30.4 us (9%)
  blocking collectives  26.4 us (8%)
  matrix products  24.1 us (7%)
  local copies, waits for them, and re-layouts  23.2 us (7%)
  between operations  15 us (4%)
  other arithmetic  14.3 us (4%)
    all_gather x3, waiting for transfers between devices, shards(): hidden = lax.all_gather(result, 'col', axis=1, tiled=True)  149 us
    ppermute x3, waiting for transfers between devices, ring_gather(): lax.ppermute(going_down, axis, [(d, (d - 1) % ways) for d in range(ways)])  39.1 us
    ppermute x3, starting transfers between devices, ring_gather(): lax.ppermute(going_down, axis, [(d, (d - 1) % ways) for d in range(ways)])  19.5 us
    dot_general x4, matrix products, shards(): jnp.dot(active, layer_weight[layer_index], preferred_element_type=jnp.flo...  19.3 us
    ppermute x4, waiting for transfers between devices, ring_gather(): lax.ppermute(going_up, axis, [(d, (d + 1) % ways) for d in range(ways)])  14 us
    psum x1, blocking collectives, shards(): row_total = lax.psum(counts, 'col')  13.1 us
    reduce_sum x4, other arithmetic, one_block(): jnp.mean(values * values, axis=1, keepdims=True) + epsilon  9.27 us
    unnamed x1, blocking collectives  8.46 us
  transfers between devices with their start and end apart: 12, of which 7 were waited for; matrix products, arithmetic and copies ran while one was open for 5% of the time, Pallas kernels for 0%

profile of v1, /device:TPU:0, one launch (start us, length us, event | category | flops | bytes accessed | tf_op | source)
XLA Modules:
  0.0 336.1 jit_solution(8455702424593576657)
XLA Ops:
  7.4 0.9 convert_reduce_fusion.1
  8.9 1.2 dynamic-slice.5
  10.9 13.1 %all-reduce.3 = (s32[8]{0:T(128)S(1)}, s32[64]{0:T(128)S(1)}) all-reduce(s32[8]{0:T(128)S(1)} %convert_reduce_fusion.2, s32[64]{0:T(128)S(1)} %dynamic-update-slice.1), channel_id=1, replica_groups=mesh['row'=4,'col'=8] {'col'}, use_global_device_ids=true, to_apply=%region_1.2 | all-reduce | flops 72 | bytes 576 | tf_op jit(solution)/shard_map/psum | solution.py:69
  24.0 1.2 dynamic-slice.4
  26.2 4.9 %all-reduce.4 = (s32[8]{0:T(128)S(1)}, s32[32]{0:T(128)S(1)}) all-reduce(s32[8]{0:T(128)S(1)} %get-tuple-element.117, s32[32]{0:T(128)S(1)} %dynamic-update-slice), channel_id=1, replica_groups=mesh['row'=4,'col'=8] {'row'}, use_global_device_ids=true, to_apply=%region_2.3 | all-reduce | flops 40 | bytes 320 | tf_op jit(solution)/shard_map/psum | solution.py:71
  33.8 3.2 all-to-all-start
  37.0 1.2 convolution_convert_fusion
  38.8 1.1 fusion.106
  40.7 3.5 %all-to-all-start.1 = ((bf16[4,16,4096]{2,1,0:T(8,128)(2,1)}), bf16[4,16,4096]{2,1,0:T(8,128)(2,1)S(1)}, u32[]{:S(2)}, u32[]{:S(2)}) async-start(bf16[4,16,4096]{2,1,0:T(8,128)(2,1)} %bitcast.8), calls=%async_computation.1 | async-start | bytes 1048576 | tf_op jit(solution)/shard_map/all_to_all | solution.py:97
  44.2 3.6 %fusion.90 = f32[256,4096]{1,0:T(8,128)} fusion(bf16[8,4096]{1,0:T(8,128)(2,1)} %param.11, s32[256]{0:T(256)S(1)} %multiply_add_fusion, s32[8]{0:T(128)S(1)} %bitcast.57, s32[8]{0:T(128)S(1)} %get-tuple-element.126), kind=kOutput, calls=%fused_computation.81 | convolution fusion | flops 16783360 | bytes 4260928 | tf_op jit(solution)/shard_map/dot_general | solution.py:114
  49.3 8.5 %all-reduce.2 = s32[512]{0:T(512)S(1)} all-reduce(s32[512]{0:T(512)S(1)} %dynamic-update-slice.2), channel_id=1, replica_groups=mesh['row'=4,'col'=8] {'col'}, use_global_device_ids=true, to_apply=%add.2 | all-reduce | flops 512 | bytes 4096
  57.7 1.6 collective-permute-start
  59.4 3.1 collective-permute-start.1
  62.5 2.5 broadcast_in_dim.71
  65.8 14.0 %collective-permute-done = bf16[64,4096]{1,0:T(8,128)(2,1)S(1)} collective-permute-done((bf16[64,4096]{1,0:T(8,128)(2,1)S(1)}, bf16[64,4096]{1,0:T(8,128)(2,1)S(1)}, u32[]{:S(2)}, u32[]{:S(2)}) %collective-permute-start) | collective-permute-done | bytes 524320 | tf_op jit(solution)/shard_map/ppermute | solution.py:17
  79.7 2.5 collective-permute-start.2
  82.2 12.9 %collective-permute-start.3 = (bf16[64,4096]{1,0:T(8,128)(2,1)S(1)}, bf16[64,4096]{1,0:T(8,128)(2,1)S(1)}, u32[]{:S(2)}, u32[]{:S(2)}) collective-permute-start(bf16[64,4096]{1,0:T(8,128)(2,1)S(1)} %collective-permute-done.1), channel_id=1, source_target_pairs={{0,7},{1,0},{2,1},{3,2},{4,3},{5,4},{6,5},{7,6},{8,15},{9,8},{10,9... | collective-permute-start | bytes 1572872 | tf_op jit(solution)/shard_map/ppermute | solution.py:20
  96.9 20.0 %collective-permute-done.3 = bf16[64,4096]{1,0:T(8,128)(2,1)S(1)} collective-permute-done((bf16[64,4096]{1,0:T(8,128)(2,1)S(1)}, bf16[64,4096]{1,0:T(8,128)(2,1)S(1)}, u32[]{:S(2)}, u32[]{:S(2)}) %collective-permute-start.3) | collective-permute-done | bytes 524320 | tf_op jit(solution)/shard_map/ppermute | solution.py:20
  116.8 3.4 %collective-permute-start.5 = (bf16[64,4096]{1,0:T(8,128)(2,1)S(1)}, bf16[64,4096]{1,0:T(8,128)(2,1)S(1)}, u32[]{:S(2)}, u32[]{:S(2)}) collective-permute-start(bf16[64,4096]{1,0:T(8,128)(2,1)S(1)} %collective-permute-done.3), channel_id=1, source_target_pairs={{0,7},{1,0},{2,1},{3,2},{4,3},{5,4},{6,5},{7,6},{8,15},{9,8},{10,9... | collective-permute-start | bytes 1572872 | tf_op jit(solution)/shard_map/ppermute | solution.py:20
  122.8 19.2 %collective-permute-done.5 = bf16[64,4096]{1,0:T(8,128)(2,1)S(1)} collective-permute-done((bf16[64,4096]{1,0:T(8,128)(2,1)S(1)}, bf16[64,4096]{1,0:T(8,128)(2,1)S(1)}, u32[]{:S(2)}, u32[]{:S(2)}) %collective-permute-start.5) | collective-permute-done | bytes 524320 | tf_op jit(solution)/shard_map/ppermute | solution.py:20
  143.6 8.4 %scatter_custom_fusion = bf16[256,4096]{1,0:T(8,128)(2,1)S(1)} fusion(s32[512]{0:T(512)S(1)} %compare_select_fusion, bf16[512,4096]{1,0:T(8,128)(2,1)} %constant_dynamic-update-slice_fusion, bf16[]{:T(256)} %constant.174.clone.1), kind=kCustom, calls=%fused_computation.71 | custom fusion | bytes 2097664 | tf_op jit(solution)/shard_map/scatter | solution.py:107
  152.0 3.0 fusion
  155.1 4.4 %add_convert_fusion.1 = bf16[256,512]{1,0:T(8,128)(2,1)} fusion(bf16[256,4096]{1,0:T(8,128)(2,1)S(1)} %get-tuple-element.122, s32[]{:T(128)S(6)} %select_n.128, bf16[4,4096,512]{2,1,0:T(8,128)(2,1)} %param.13, f32[4096]{0:T(1024)S(1)} %bitcast.56, f32[256]{0:T(256)S(1)} %add_rsqrt_fusion.3), kind=kOutput, calls=%fused_computation.73 | convolution fusion | flops 1082523648 | bytes 6833156 | tf_op jit(solution)/shard_map/dot_general | solution.py:124
  159.5 51.4 %all-gather.6.cloned.1.call-done = bf16[256,4096]{1,0:T(8,128)(2,1)} async-done(((bf16[256,512]{1,0:T(8,128)(2,1)}), bf16[256,4096]{1,0:T(8,128)(2,1)}) %all-gather.6.cloned.1.call-update) | async-done | bytes 2097168 | tf_op jit(solution)/shard_map/all_gather | solution.py:128
  210.9 2.1 fusion.8
  213.0 5.0 %fusion.81 = bf16[256,512]{1,0:T(8,128)(2,1)} fusion(bf16[4,4096,512]{2,1,0:T(8,128)(2,1)} %param.13, bf16[256,4096]{1,0:T(8,128)(2,1)} %all-gather.6.cloned.1.call-done, f32[4096]{0:T(1024)S(1)} %bitcast.55, f32[256]{0:T(256)S(1)} %add_rsqrt_fusion.2, s32[]{:T(128)S(6)} %select_n.128), kind=kOutput, calls=%fused_computation.70 | convolution fusion | flops 1082523648 | bytes 6833156 | tf_op jit(solution)/shard_map/dot_general | solution.py:124
  218.1 48.6 %all-gather.8.cloned.1.call-done = bf16[256,4096]{1,0:T(8,128)(2,1)} async-done(((bf16[256,512]{1,0:T(8,128)(2,1)}), bf16[256,4096]{1,0:T(8,128)(2,1)}) %all-gather.8.cloned.1.call-update) | async-done | bytes 2097168 | tf_op jit(solution)/shard_map/all_gather | solution.py:128
  266.7 2.1 fusion.16
  268.8 5.0 %fusion.76 = bf16[256,512]{1,0:T(8,128)(2,1)} fusion(bf16[4,4096,512]{2,1,0:T(8,128)(2,1)} %param.13, bf16[256,4096]{1,0:T(8,128)(2,1)} %all-gather.8.cloned.1.call-done, f32[4096]{0:T(1024)S(1)} %bitcast.54, f32[256]{0:T(256)S(1)} %add_rsqrt_fusion.1, s32[]{:T(128)S(6)} %select_n.128), kind=kOutput, calls=%fused_computation.69 | convolution fusion | flops 1082523648 | bytes 6833156 | tf_op jit(solution)/shard_map/dot_general | solution.py:124
  273.8 48.8 %all-gather.10.cloned.1.call-done = bf16[256,4096]{1,0:T(8,128)(2,1)} async-done(((bf16[256,512]{1,0:T(8,128)(2,1)}), bf16[256,4096]{1,0:T(8,128)(2,1)}) %all-gather.10.cloned.1.call-update) | async-done | bytes 2097168 | tf_op jit(solution)/shard_map/all_gather | solution.py:128
  322.5 2.1 fusion.24
  324.6 5.0 %fusion.71 = bf16[256,512]{1,0:T(8,128)(2,1)} fusion(bf16[4,4096,512]{2,1,0:T(8,128)(2,1)} %param.13, bf16[256,4096]{1,0:T(8,128)(2,1)} %all-gather.10.cloned.1.call-done, f32[4096]{0:T(1024)S(1)} %bitcast.53, f32[256]{0:T(256)S(1)} %add_rsqrt_fusion, s32[]{:T(128)S(6)} %select_n.128), kind=kOutput, calls=%fused_computation.68 | convolution fusion | flops 1082523648 | bytes 6833156 | tf_op jit(solution)/shard_map/dot_general | solution.py:124
  (56 shorter events, 13.9 us)
Async XLA Ops:
  6.5 30.5 %copy-start = (bf16[32,4096]{1,0:T(8,128)(2,1)S(1)}, bf16[32,4096]{1,0:T(8,128)(2,1)}, u32[]{:S(2)}) copy-start(bf16[32,4096]{1,0:T(8,128)(2,1)} %param.9) | copy-start | bytes 786436
  33.8 6.9 %all-to-all-start = ((s32[4,1,16]{2,1,0:T(1,128)}), s32[4,1,16]{2,1,0:T(1,128)S(1)}, u32[]{:S(2)}, u32[]{:S(2)}) async-start(s32[4,1,16]{2,1,0:T(1,128)} %bitcast.6), calls=%async_computation | async-start | bytes 4096 | tf_op jit(solution)/shard_map/all_to_all | solution.py:98
  40.7 17.0 %all-to-all-start.1 = ((bf16[4,16,4096]{2,1,0:T(8,128)(2,1)}), bf16[4,16,4096]{2,1,0:T(8,128)(2,1)S(1)}, u32[]{:S(2)}, u32[]{:S(2)}) async-start(bf16[4,16,4096]{2,1,0:T(8,128)(2,1)} %bitcast.8), calls=%async_computation.1 | async-start | bytes 1048576 | tf_op jit(solution)/shard_map/all_to_all | solution.py:97
  44.2 166.7 %all-gather.6.cloned.1.call-start = ((), (), s32[]{:S(2)}) async-start(), calls=%async_computation.2 | async-start | bytes 2359296 | tf_op jit(solution)/shard_map/all_gather | solution.py:128
  57.7 22.0 %collective-permute-start = (bf16[64,4096]{1,0:T(8,128)(2,1)S(1)}, bf16[64,4096]{1,0:T(8,128)(2,1)S(1)}, u32[]{:S(2)}, u32[]{:S(2)}) collective-permute-start(bf16[64,4096]{1,0:T(8,128)(2,1)S(1)} %bitcast.50), channel_id=1, source_target_pairs={{0,1},{1,2},{2,3},{3,4},{4,5},{5,6},{6,7},{7,0},{8,9},{9,10},{10,1... | collective-permute-start | bytes 1572872 | tf_op jit(solution)/shard_map/ppermute | solution.py:17
  59.4 22.9 %collective-permute-start.1 = (bf16[64,4096]{1,0:T(8,128)(2,1)S(1)}, bf16[64,4096]{1,0:T(8,128)(2,1)S(1)}, u32[]{:S(2)}, u32[]{:S(2)}) collective-permute-start(bf16[64,4096]{1,0:T(8,128)(2,1)S(1)} %bitcast.51), channel_id=1, source_target_pairs={{0,7},{1,0},{2,1},{3,2},{4,3},{5,4},{6,5},{7,6},{8,15},{9,8},{10,9... | collective-permute-start | bytes 1572872 | tf_op jit(solution)/shard_map/ppermute | solution.py:20
  79.7 17.1 %collective-permute-start.2 = (bf16[64,4096]{1,0:T(8,128)(2,1)S(1)}, bf16[64,4096]{1,0:T(8,128)(2,1)S(1)}, u32[]{:S(2)}, u32[]{:S(2)}) collective-permute-start(bf16[64,4096]{1,0:T(8,128)(2,1)S(1)} %collective-permute-done), channel_id=1, source_target_pairs={{0,1},{1,2},{2,3},{3,4},{4,5},{5,6},{6,7},{7,0},{8,9},{9,10},{10,1... | collective-permute-start | bytes 1572872 | tf_op jit(solution)/shard_map/ppermute | solution.py:17
  82.2 34.6 %collective-permute-start.3 = (bf16[64,4096]{1,0:T(8,128)(2,1)S(1)}, bf16[64,4096]{1,0:T(8,128)(2,1)S(1)}, u32[]{:S(2)}, u32[]{:S(2)}) collective-permute-start(bf16[64,4096]{1,0:T(8,128)(2,1)S(1)} %collective-permute-done.1), channel_id=1, source_target_pairs={{0,7},{1,0},{2,1},{3,2},{4,3},{5,4},{6,5},{7,6},{8,15},{9,8},{10,9... | collective-permute-start | bytes 1572872 | tf_op jit(solution)/shard_map/ppermute | solution.py:20
  96.9 25.0 %collective-permute-start.4 = (bf16[64,4096]{1,0:T(8,128)(2,1)S(1)}, bf16[64,4096]{1,0:T(8,128)(2,1)S(1)}, u32[]{:S(2)}, u32[]{:S(2)}) collective-permute-start(bf16[64,4096]{1,0:T(8,128)(2,1)S(1)} %collective-permute-done.2), channel_id=1, source_target_pairs={{0,1},{1,2},{2,3},{3,4},{4,5},{5,6},{6,7},{7,0},{8,9},{9,10},{10,1... | collective-permute-start | bytes 1572872 | tf_op jit(solution)/shard_map/ppermute | solution.py:17
  116.8 25.1 %collective-permute-start.5 = (bf16[64,4096]{1,0:T(8,128)(2,1)S(1)}, bf16[64,4096]{1,0:T(8,128)(2,1)S(1)}, u32[]{:S(2)}, u32[]{:S(2)}) collective-permute-start(bf16[64,4096]{1,0:T(8,128)(2,1)S(1)} %collective-permute-done.3), channel_id=1, source_target_pairs={{0,7},{1,0},{2,1},{3,2},{4,3},{5,4},{6,5},{7,6},{8,15},{9,8},{10,9... | collective-permute-start | bytes 1572872 | tf_op jit(solution)/shard_map/ppermute | solution.py:20
  121.9 20.9 %collective-permute-start.6 = (bf16[64,4096]{1,0:T(8,128)(2,1)S(1)}, bf16[64,4096]{1,0:T(8,128)(2,1)S(1)}, u32[]{:S(2)}, u32[]{:S(2)}) collective-permute-start(bf16[64,4096]{1,0:T(8,128)(2,1)S(1)} %collective-permute-done.4), channel_id=1, source_target_pairs={{0,1},{1,2},{2,3},{3,4},{4,5},{5,6},{6,7},{7,0},{8,9},{9,10},{10,1... | collective-permute-start | bytes 1572872 | tf_op jit(solution)/shard_map/ppermute | solution.py:17
  159.4 107.3 %all-gather.8.cloned.1.call-start = ((), (), s32[]{:S(2)}) async-start(), calls=%async_computation.3 | async-start | bytes 2359296 | tf_op jit(solution)/shard_map/all_gather | solution.py:128
  218.0 104.5 %all-gather.10.cloned.1.call-start = ((), (), s32[]{:S(2)}) async-start(), calls=%async_computation.4 | async-start | bytes 2359296 | tf_op jit(solution)/shard_map/all_gather | solution.py:128
Sparse Core Ops, SparseCore 0:
  159.5 51.3 all-gather.5
  218.1 48.5 all-gather.7
  273.9 48.5 all-gather.9
